TPU v7x, 256 devices: a whole 4x4x8 slice. The times are simulated.
256 devices in a mesh: lvl: 4 (over y), gz: 32 (over z_hi, x, core), gy: 2 (over z_lo).
Axes of the slice: x: 4, y: 4, z: 8 (z_hi: 4, z_lo: 2; z = z_hi * 2 + z_lo), core: 2. Of those that a mesh axis runs over, the one named last changes fastest.
Arguments:
- fine_field: float32 [256, 512, 1024], P('gz', 'gy', 'lvl'), may hold values from -1.2 to 1.2
- noise_pair: float32 [2, 256, 512, 1024], P(None, 'gz', 'gy', 'lvl'), may hold values from -4 to 4
Outputs:
- fine_next: float32 [256, 512, 1024], P('gz', 'gy', 'lvl')
- correction: float32 [128, 256, 512], P('gz', 'gy', 'lvl')
All inputs are finite; a program needn't handle non-finite values.
Results may differ from a plain program's by a relative error of at most 0.00014.
Values sent between devices are 32-bit elements; how exact they have to be, the bound alone decides.
No kernel may reach another device: no remote copies, remote signals or barrier semaphores. Data moves between devices by JAX's collectives and lax.ppermute only.
A program may use at most 64 MiB of HBM per device.

v0:
```python
import jax
import jax.numpy as jnp
from jax import lax
from jax.sharding import PartitionSpec as P

noise_amp = 0.3


def padded_2(cells, sides, width):
    for axis, dim in sides:
        count = lax.axis_size(axis)
        head = lax.slice_in_dim(cells, 0, width, axis=dim)
        tail = lax.slice_in_dim(cells, cells.shape[dim] - width, cells.shape[dim], axis=dim)
        cells = jnp.concatenate(
            [
                lax.ppermute(tail, axis, [(i, (i + 1) % count) for i in range(count)]),
                cells,
                lax.ppermute(head, axis, [((i + 1) % count, i) for i in range(count)]),
            ],
            axis=dim,
        )
    return cells


def neighbours(padded):
    beside = padded[2:, 1:-1, 1:-1] + padded[:-2, 1:-1, 1:-1]
    beside = beside + padded[1:-1, 2:, 1:-1] + padded[1:-1, :-2, 1:-1]
    beside = beside + padded[1:-1, 1:-1, 2:] + padded[1:-1, 1:-1, :-2]
    return beside


def advance(padded, forcing, spread, react):
    center = padded[1:-1, 1:-1, 1:-1]
    return (
        center
        + spread * (neighbours(padded) - 6.0 * center)
        + react * (center - center * center * center)
        + noise_amp * forcing
    )


def coarsen(values):
    first, second, third = values.shape
    half = third // 2
    source = lax.broadcasted_iota(jnp.int32, (third, half), 0) // 2
    target = lax.broadcasted_iota(jnp.int32, (third, half), 1)
    table = (source == target).astype(jnp.float32)
    paired = jnp.dot(
        values.reshape(first * second, third),
        table,
        precision=lax.Precision.HIGHEST,
        preferred_element_type=jnp.float32,
    )
    paired = paired.reshape(first // 2, 2, second // 2, 2 * half)
    summed = paired[:, 0] + paired[:, 1]
    return (summed[:, :, :half] + summed[:, :, half:]) * 0.125


def fine_rim(values):
    return padded_2(values, (("lvl", 2), ("gz", 0), ("gy", 1)), 1)


def on_device(fine_field, noise_pair):
    coarse_padded = None
    middle = advance(fine_rim(fine_field), noise_pair[0], 0.15, 0.1)
    fine_next = advance(fine_rim(middle), noise_pair[1], 0.15, 0.1)
    coarse_noise = coarsen(noise_pair[0] + noise_pair[1])
    coarse_start = coarsen(fine_field)
    coarse_padded = padded_2(coarse_start, (("lvl", 2), ("gz", 0), ("gy", 1)), 1)
    coarse_next = advance(coarse_padded, coarse_noise, 0.075, 0.2)
    return (fine_next, coarsen(fine_next) - coarse_next)


def solution(mesh):
    in_specs = (P("gz", "gy", "lvl"), P(None, "gz", "gy", "lvl"))
    out_specs = (P("gz", "gy", "lvl"), P("gz", "gy", "lvl"))
    return jax.shard_map(
        on_device, mesh=mesh, in_specs=in_specs, out_specs=out_specs, check_vma=False
    )
```

profile of v0, /device:TPU:32, one launch (start us, length us, event | category | flops | bytes accessed | tf_op | source)
XLA Modules:
  0.0 96.1 jit_solution(3316683565125044639)
XLA Ops:
  0.6 2.9 %fusion.55 = (f32[8,256,1]{2,1,0:T(8,128)S(1)}, f32[8,256,1]{2,1,0:T(8,128)}) fusion(f32[8,256,256]{2,1,0:T(8,128)} %param.2), kind=kLoop, calls=%fused_computation.152 | loop fusion | bytes 32768 | tf_op jit(solution)/shard_map/slice | solution.py:12
  3.5 1.7 %copy.49 = f32[8,256,1]{1,0,2:T(8,128)S(1)} copy(f32[8,256,1]{2,1,0:T(8,128)} %get-tuple-element.15) | data formatting | bytes 16384
  5.2 1.6 %collective-permute-start = (f32[8,256,1]{1,0,2:T(8,128)S(1)}, f32[8,256,1]{1,0,2:T(8,128)S(1)}, u32[]{:S(2)}, u32[]{:S(2)}) collective-permute-start(f32[8,256,1]{1,0,2:T(8,128)S(1)} %copy.49), channel_id=1, source_target_pairs={{0,64},{64,128},{128,192},{192,0},{1,65},{65,129},{129,193},{193,1... | collective-permute-start | bytes 24584 | tf_op jit(solution)/shard_map/ppermute | solution.py:16
  6.8 0.3 copy.50
  7.1 1.7 %collective-permute-start.1 = (f32[8,256,1]{1,0,2:T(8,128)S(1)}, f32[8,256,1]{1,0,2:T(8,128)S(1)}, u32[]{:S(2)}, u32[]{:S(2)}) collective-permute-start(f32[8,256,1]{1,0,2:T(8,128)S(1)} %copy.50), channel_id=1, source_target_pairs={{64,0},{128,64},{192,128},{0,192},{65,1},{129,65},{193,129},{1,193... | collective-permute-start | bytes 24584 | tf_op jit(solution)/shard_map/ppermute | solution.py:18
  8.9 1.4 %convolution_bitcast_fusion = f32[2048,128]{0,1:T(8,128)S(1)} fusion(f32[2048,256]{1,0:T(8,128)S(1)} %bitcast.38, s32[256]{0:T(256)S(1)} %get-tuple-element.22, s32[256]{0:T(256)S(1)} %get-tuple-element.23, pred[256]{0:T(512)(128)(4,1)S(1)} %compare_and_fusion), kind=kOutput, calls=%fused_computation.2 | convolution fusion | flops 805404672 | bytes 3148032 | tf_op jit(solution)/shard_map/dot_general | solution.py:48
  10.3 1.3 %copy.46 = f32[2048,128]{1,0:T(8,128)} copy(f32[2048,128]{0,1:T(8,128)S(1)} %convolution_bitcast_fusion) | data formatting | bytes 2097152 | tf_op jit(solution)/shard_map/dot_general | solution.py:48
  11.6 1.5 %reshape.33 = f32[4,2,128,256]{3,2,1,0:T(8,128)S(1)} reshape(f32[2048,128]{1,0:T(8,128)} %copy.46) | data formatting | bytes 2097152 | tf_op jit(solution)/shard_map/reshape | solution.py:54
  13.1 0.9 fusion.24
  14.0 0.4 copy.34
  14.4 1.3 %copy.35 = f32[8,256,1]{2,1,0:T(8,128)} copy(f32[8,256,1]{1,0,2:T(8,128)S(1)} %collective-permute-done.1) | data formatting | bytes 16384 | tf_op jit(solution)/shard_map/ppermute | solution.py:18
  15.7 1.4 %pad_maximum_fusion.39 = (f32[1,256,258]{2,1,0:T(8,128)S(1)}, f32[1,256,258]{2,1,0:T(8,128)S(1)}) fusion(f32[8,256,1]{2,1,0:T(8,128)} %copy.35, f32[8,256,256]{2,1,0:T(8,128)S(1)} %copy-done, f32[8,256,1]{2,1,0:T(8,128)S(1)} %copy.34), kind=kLoop, calls=%fused_computation.75 | loop fusion | flops 264192 | bytes 2641920 | tf_op jit(solution)/shard_map/concatenate | solution.py:14
  17.1 6.6 %collective-permute-start.2 = (f32[1,256,258]{2,1,0:T(8,128)S(1)}, f32[1,256,258]{2,1,0:T(8,128)S(1)}, u32[]{:S(2)}, u32[]{:S(2)}) collective-permute-start(f32[1,256,258]{2,1,0:T(8,128)S(1)} %get-tuple-element.11), channel_id=1, source_target_pairs={{2,0},{4,2},{6,4},{8,6},{10,8},{12,10},{14,12},{16,14},{18,16},{20... | collective-permute-start | bytes 792584 | tf_op jit(solution)/shard_map/ppermute | solution.py:18
  23.8 0.9 fusion.56
  24.9 2.9 %collective-permute-start.13 = (f32[4,128,1]{2,1,0:T(8,128)}, f32[4,128,1]{2,1,0:T(8,128)}, u32[]{:S(2)}, u32[]{:S(2)}) collective-permute-start(f32[4,128,1]{2,1,0:T(8,128)} %get-tuple-element.20), channel_id=1, source_target_pairs={{64,0},{128,64},{192,128},{0,192},{65,1},{129,65},{193,129},{1,193... | collective-permute-start | bytes 6152 | tf_op jit(solution)/shard_map/ppermute | solution.py:18
  27.9 3.9 %collective-permute-done.2 = f32[1,256,258]{2,1,0:T(8,128)S(1)} collective-permute-done((f32[1,256,258]{2,1,0:T(8,128)S(1)}, f32[1,256,258]{2,1,0:T(8,128)S(1)}, u32[]{:S(2)}, u32[]{:S(2)}) %collective-permute-start.2) | collective-permute-done | bytes 264224 | tf_op jit(solution)/shard_map/ppermute | solution.py:18
  31.8 5.8 %collective-permute-done.3 = f32[1,256,258]{2,1,0:T(8,128)S(1)} collective-permute-done((f32[1,256,258]{2,1,0:T(8,128)S(1)}, f32[1,256,258]{2,1,0:T(8,128)S(1)}, u32[]{:S(2)}, u32[]{:S(2)}) %collective-permute-start.3) | collective-permute-done | bytes 264224 | tf_op jit(solution)/shard_map/ppermute | solution.py:16
  37.8 2.6 %collective-permute-start.5 = (f32[10,1,258]{2,1,0:T(1,128)S(1)}, f32[10,1,258]{2,1,0:T(1,128)S(1)}, u32[]{:S(2)}, u32[]{:S(2)}) collective-permute-start(f32[10,1,258]{2,1,0:T(1,128)S(1)} %get-tuple-element.7), channel_id=1, source_target_pairs={{0,1},{1,0},{2,3},{3,2},{4,5},{5,4},{6,7},{7,6},{8,9},{9,8},{10,11... | collective-permute-start | bytes 30968 | tf_op jit(solution)/shard_map/ppermute | solution.py:16
  40.5 1.6 %slice_add_fusion = f32[1,8,256,256]{3,2,1,0:T(8,128)} fusion(f32[2,8,256,256]{3,2,1,0:T(8,128)S(1)} %copy-done.3), kind=kLoop, calls=%fused_computation.61 | loop fusion | flops 524288 | bytes 6291456 | tf_op jit(solution)/shard_map/add | solution.py:67
  42.2 2.0 %collective-permute-done.4 = f32[10,1,258]{2,1,0:T(1,128)S(1)} collective-permute-done((f32[10,1,258]{2,1,0:T(1,128)S(1)}, f32[10,1,258]{2,1,0:T(1,128)S(1)}, u32[]{:S(2)}, u32[]{:S(2)}) %collective-permute-start.4) | collective-permute-done | bytes 10352 | tf_op jit(solution)/shard_map/ppermute | solution.py:18
  44.1 5.0 %fusion.2 = f32[8,256,256]{2,1,0:T(8,128)S(1)} fusion(f32[8,256,256]{2,1,0:T(8,128)S(1)} %copy-done, f32[8,256,1]{2,1,0:T(8,128)S(1)} %copy.34, f32[8,256,1]{2,1,0:T(8,128)S(1)} %copy-done.6, f32[10,1,258]{2,1,0:T(1,128)S(1)} %collective-permute-done.5, f32[1,256,258]{2,1,0:T(8,128)S(1)} %collective-permute-done.2, ...), kind=kLoop, calls=%fused_computation.5 | loop fusion | flops 17825792 | bytes 6856864 | tf_op jit(solution)/shard_map/add | solution.py:35
  49.1 1.6 %fusion.54 = (f32[8,256,1]{2,1,0:T(8,128)S(1)}, f32[8,256,1]{2,1,0:T(8,128)}) fusion(f32[8,256,256]{2,1,0:T(8,128)S(1)} %fusion.2), kind=kLoop, calls=%fused_computation.151 | loop fusion | bytes 32768 | tf_op jit(solution)/shard_map/slice | solution.py:12
  50.8 1.7 %copy.38 = f32[8,256,1]{1,0,2:T(8,128)S(1)} copy(f32[8,256,1]{2,1,0:T(8,128)} %get-tuple-element.13) | data formatting | bytes 16384 | tf_op jit(solution)/shard_map/slice | solution.py:13
  52.5 0.3 collective-permute-start.6
  52.8 0.3 copy.39
  53.2 3.2 %collective-permute-start.7 = (f32[8,256,1]{1,0,2:T(8,128)S(1)}, f32[8,256,1]{1,0,2:T(8,128)S(1)}, u32[]{:S(2)}, u32[]{:S(2)}) collective-permute-start(f32[8,256,1]{1,0,2:T(8,128)S(1)} %copy.39), channel_id=1, source_target_pairs={{64,0},{128,64},{192,128},{0,192},{65,1},{129,65},{193,129},{1,193... | collective-permute-start | bytes 24584 | tf_op jit(solution)/shard_map/ppermute | solution.py:18
  56.3 1.2 %fusion.41 = f32[2048,128]{1,0:T(8,128)S(1)} fusion(f32[2048,256]{1,0:T(8,128)S(1)} %bitcast.39, s32[256]{0:T(256)S(1)} %get-tuple-element.22, s32[256]{0:T(256)S(1)} %get-tuple-element.23, pred[256]{0:T(512)(128)(4,1)S(1)} %compare_and_fusion), kind=kOutput, calls=%fused_computation.119 | convolution fusion | flops 805371904 | bytes 3148032 | tf_op jit(solution)/shard_map/dot_general | solution.py:48
  57.5 1.3 %reshape.34 = f32[4,2,128,256]{3,2,1,0:T(8,128)} reshape(f32[2048,128]{1,0:T(8,128)S(1)} %fusion.41) | data formatting | bytes 2097152 | tf_op jit(solution)/shard_map/reshape | solution.py:54
  58.8 0.4 copy.40
  59.2 1.4 %copy.41 = f32[8,256,1]{2,1,0:T(8,128)} copy(f32[8,256,1]{1,0,2:T(8,128)S(1)} %collective-permute-done.7) | data formatting | bytes 16384 | tf_op jit(solution)/shard_map/ppermute | solution.py:18
  60.6 1.4 %pad_maximum_fusion.36 = (f32[1,256,258]{2,1,0:T(8,128)S(1)}, f32[1,256,258]{2,1,0:T(8,128)S(1)}) fusion(f32[8,256,1]{2,1,0:T(8,128)} %copy.41, f32[8,256,256]{2,1,0:T(8,128)S(1)} %copy-done.2, f32[8,256,1]{2,1,0:T(8,128)S(1)} %copy.40), kind=kLoop, calls=%fused_computation.72 | loop fusion | flops 264192 | bytes 2641920 | tf_op jit(solution)/shard_map/concatenate | solution.py:14
  62.1 0.5 collective-permute-start.9
  62.6 0.9 fusion.23
  63.4 1.1 %pad_maximum_fusion.60 = (f32[1,128,130]{2,1,0:T(8,128)S(1)}, f32[1,128,130]{2,1,0:T(8,128)S(1)}) fusion(f32[4,128,1]{2,1,0:T(8,128)} %collective-permute-done.13, f32[4,128,128]{2,1,0:T(8,128)S(1)} %broadcast_multiply_fusion, f32[4,128,1]{2,1,0:T(8,128)} %collective-permute-done.12), kind=kLoop, calls=%fused_computation.114 | loop fusion | flops 66560 | bytes 399360 | tf_op jit(solution)/shard_map/concatenate | solution.py:14
  64.5 5.6 %collective-permute-start.14 = (f32[1,128,130]{2,1,0:T(8,128)S(1)}, f32[1,128,130]{2,1,0:T(8,128)S(1)}, u32[]{:S(2)}, u32[]{:S(2)}) collective-permute-start(f32[1,128,130]{2,1,0:T(8,128)S(1)} %get-tuple-element.19), channel_id=1, source_target_pairs={{2,0},{4,2},{6,4},{8,6},{10,8},{12,10},{14,12},{16,14},{18,16},{20... | collective-permute-start | bytes 199688 | tf_op jit(solution)/shard_map/ppermute | solution.py:18
  70.2 2.3 %collective-permute-done.8 = f32[1,256,258]{2,1,0:T(8,128)S(1)} collective-permute-done((f32[1,256,258]{2,1,0:T(8,128)S(1)}, f32[1,256,258]{2,1,0:T(8,128)S(1)}, u32[]{:S(2)}, u32[]{:S(2)}) %collective-permute-start.8) | collective-permute-done | bytes 264224 | tf_op jit(solution)/shard_map/ppermute | solution.py:18
  72.5 3.8 %collective-permute-done.9 = f32[1,256,258]{2,1,0:T(8,128)S(1)} collective-permute-done((f32[1,256,258]{2,1,0:T(8,128)S(1)}, f32[1,256,258]{2,1,0:T(8,128)S(1)}, u32[]{:S(2)}, u32[]{:S(2)}) %collective-permute-start.9) | collective-permute-done | bytes 264224 | tf_op jit(solution)/shard_map/ppermute | solution.py:16
  76.4 3.6 %collective-permute-start.11 = (f32[10,1,258]{2,1,0:T(1,128)S(1)}, f32[10,1,258]{2,1,0:T(1,128)S(1)}, u32[]{:S(2)}, u32[]{:S(2)}) collective-permute-start(f32[10,1,258]{2,1,0:T(1,128)S(1)} %get-tuple-element.5), channel_id=1, source_target_pairs={{0,1},{1,0},{2,3},{3,2},{4,5},{5,4},{6,7},{7,6},{8,9},{9,8},{10,11... | collective-permute-start | bytes 30968 | tf_op jit(solution)/shard_map/ppermute | solution.py:16
  80.1 0.9 collective-permute-done.15
  81.0 1.5 %pad_maximum_fusion.77 = (f32[6,1,130]{2,1,0:T(1,128)S(1)}, f32[6,1,130]{2,1,0:T(1,128)}) fusion(f32[1,128,130]{2,1,0:T(8,128)S(1)} %collective-permute-done.14, f32[1,128,130]{2,1,0:T(8,128)S(1)} %collective-permute-done.15, f32[4,128,1]{2,1,0:T(8,128)} %collective-permute-done.13, f32[4,128,128]{2,1,0:T(8,128)S(1)} %broadcast_multiply_fusion, ...), kind=kLoop, calls=%fused_computation.145 | loop fusion | flops 6240 | bytes 405600 | tf_op jit(solution)/shard_map/slice | solution.py:12
  82.5 1.0 %collective-permute-start.17 = (f32[6,1,130]{2,1,0:T(1,128)}, f32[6,1,130]{2,1,0:T(1,128)}, u32[]{:S(2)}, u32[]{:S(2)}) collective-permute-start(f32[6,1,130]{2,1,0:T(1,128)} %get-tuple-element.17), channel_id=1, source_target_pairs={{0,1},{1,0},{2,3},{3,2},{4,5},{5,4},{6,7},{7,6},{8,9},{9,8},{10,11... | collective-permute-start | bytes 9368 | tf_op jit(solution)/shard_map/ppermute | solution.py:16
  83.5 1.0 %collective-permute-start.16 = (f32[6,1,130]{2,1,0:T(1,128)S(1)}, f32[6,1,130]{2,1,0:T(1,128)}, u32[]{:S(2)}, u32[]{:S(2)}) collective-permute-start(f32[6,1,130]{2,1,0:T(1,128)S(1)} %get-tuple-element.16), channel_id=1, source_target_pairs={{1,0},{0,1},{3,2},{2,3},{5,4},{4,5},{7,6},{6,7},{9,8},{8,9},{11,10... | collective-permute-start | bytes 9368 | tf_op jit(solution)/shard_map/ppermute | solution.py:18
  84.6 5.0 %fusion.5 = f32[8,256,256]{2,1,0:T(8,128)S(1)} fusion(f32[8,256,256]{2,1,0:T(8,128)S(1)} %copy-done.2, f32[8,256,1]{2,1,0:T(8,128)S(1)} %copy.40, f32[8,256,1]{2,1,0:T(8,128)S(1)} %copy-done.5, f32[10,1,258]{2,1,0:T(1,128)S(1)} %collective-permute-done.11, f32[1,256,258]{2,1,0:T(8,128)S(1)} %collective-permute-done.8, ...), kind=kLoop, calls=%fused_computation.8 | loop fusion | flops 17825792 | bytes 6856864 | tf_op jit(solution)/shard_map/add | solution.py:35
  89.6 1.3 %copy-done.8 = f32[8,256,256]{2,1,0:T(8,128)} copy-done((f32[8,256,256]{2,1,0:T(8,128)}, f32[8,256,256]{2,1,0:T(8,128)S(1)}, u32[]{:S(2)}) %copy-start.8) | copy-done | bytes 2097176
  90.9 1.2 %fusion.43 = f32[2048,128]{1,0:T(8,128)S(1)} fusion(f32[2048,256]{1,0:T(8,128)S(1)} %bitcast.40, s32[256]{0:T(256)S(1)} %get-tuple-element.22, s32[256]{0:T(256)S(1)} %get-tuple-element.23, pred[256]{0:T(512)(128)(4,1)S(1)} %copy-done.15), kind=kOutput, calls=%fused_computation.121 | convolution fusion | flops 805371904 | bytes 3148032 | tf_op jit(solution)/shard_map/dot_general | solution.py:48
  92.2 0.3 reshape.31
  92.6 0.6 copy-done.10
  93.3 2.8 %fusion.30 = f32[4,128,128]{2,1,0:T(8,128)} fusion(f32[4,128,128]{2,1,0:T(8,128)S(1)} %broadcast_multiply_fusion, f32[4,128,256]{2,1,0:T(8,128)S(1)} %copy-done.12, f32[4,128,1]{2,1,0:T(8,128)} %collective-permute-done.12, f32[4,128,1]{2,1,0:T(8,128)} %collective-permute-done.13, f32[6,1,130]{2,1,0:T(1,128)} %collective-permute-done.17, ...), kind=kLoop, calls=%fused_computation.82 | loop fusion | flops 2555904 | bytes 2240608 | tf_op jit(solution)/shard_map/sub | solution.py:71
  (54 shorter events, 1.3 us)
Async XLA Ops:
  3.5 5.4 %copy-start = (f32[8,256,256]{2,1,0:T(8,128)S(1)}, f32[8,256,256]{2,1,0:T(8,128)}, u32[]{:S(2)}) copy-start(f32[8,256,256]{2,1,0:T(8,128)} %param.2) | copy-start | bytes 6291460
  5.2 8.8 %collective-permute-start = (f32[8,256,1]{1,0,2:T(8,128)S(1)}, f32[8,256,1]{1,0,2:T(8,128)S(1)}, u32[]{:S(2)}, u32[]{:S(2)}) collective-permute-start(f32[8,256,1]{1,0,2:T(8,128)S(1)} %copy.49), channel_id=1, source_target_pairs={{0,64},{64,128},{128,192},{192,0},{1,65},{65,129},{129,193},{193,1... | collective-permute-start | bytes 24584 | tf_op jit(solution)/shard_map/ppermute | solution.py:16
  7.1 7.2 %collective-permute-start.1 = (f32[8,256,1]{1,0,2:T(8,128)S(1)}, f32[8,256,1]{1,0,2:T(8,128)S(1)}, u32[]{:S(2)}, u32[]{:S(2)}) collective-permute-start(f32[8,256,1]{1,0,2:T(8,128)S(1)} %copy.50), channel_id=1, source_target_pairs={{64,0},{128,64},{192,128},{0,192},{65,1},{129,65},{193,129},{1,193... | collective-permute-start | bytes 24584 | tf_op jit(solution)/shard_map/ppermute | solution.py:18
  8.9 47.5 %copy-start.14 = (pred[256]{0:T(512)(128)(4,1)}, pred[256]{0:T(512)(128)(4,1)S(1)}, u32[]{:S(2)}) copy-start(pred[256]{0:T(512)(128)(4,1)S(1)} %compare_and_fusion) | copy-start | bytes 772
  15.7 8.0 %copy-start.9 = (f32[4,128,256]{2,1,0:T(8,128)S(1)}, f32[4,128,256]{2,1,0:T(8,128)}, u32[]{:S(2)}) copy-start(f32[4,128,256]{2,1,0:T(8,128)} %fusion.24) | copy-start | bytes 1572868
  17.1 20.5 %copy-start.6 = (f32[8,256,1]{2,1,0:T(8,128)S(1)}, f32[8,256,1]{2,1,0:T(8,128)}, u32[]{:S(2)}) copy-start(f32[8,256,1]{2,1,0:T(8,128)} %copy.35) | copy-start | bytes 24580
  17.1 14.7 %collective-permute-start.2 = (f32[1,256,258]{2,1,0:T(8,128)S(1)}, f32[1,256,258]{2,1,0:T(8,128)S(1)}, u32[]{:S(2)}, u32[]{:S(2)}) collective-permute-start(f32[1,256,258]{2,1,0:T(8,128)S(1)} %get-tuple-element.11), channel_id=1, source_target_pairs={{2,0},{4,2},{6,4},{8,6},{10,8},{12,10},{14,12},{16,14},{18,16},{20... | collective-permute-start | bytes 792584 | tf_op jit(solution)/shard_map/ppermute | solution.py:18
  23.7 13.9 %collective-permute-start.3 = (f32[1,256,258]{2,1,0:T(8,128)S(1)}, f32[1,256,258]{2,1,0:T(8,128)S(1)}, u32[]{:S(2)}, u32[]{:S(2)}) collective-permute-start(f32[1,256,258]{2,1,0:T(8,128)S(1)} %get-tuple-element.10), channel_id=1, source_target_pairs={{0,2},{2,4},{4,6},{6,8},{8,10},{10,12},{12,14},{14,16},{16,18},{18... | collective-permute-start | bytes 792584 | tf_op jit(solution)/shard_map/ppermute | solution.py:16
  24.6 38.8 %collective-permute-start.12 = (f32[4,128,1]{2,1,0:T(8,128)}, f32[4,128,1]{2,1,0:T(8,128)}, u32[]{:S(2)}, u32[]{:S(2)}) collective-permute-start(f32[4,128,1]{2,1,0:T(8,128)} %get-tuple-element.21), channel_id=1, source_target_pairs={{0,64},{64,128},{128,192},{192,0},{1,65},{65,129},{129,193},{193,1... | collective-permute-start | bytes 6152 | tf_op jit(solution)/shard_map/ppermute | solution.py:16
  24.9 15.6 %copy-start.3 = (f32[2,8,256,256]{3,2,1,0:T(8,128)S(1)}, f32[2,8,256,256]{3,2,1,0:T(8,128)}, u32[]{:S(2)}) copy-start(f32[2,8,256,256]{3,2,1,0:T(8,128)} %param.3) | copy-start | bytes 12582916
  24.9 38.5 %collective-permute-start.13 = (f32[4,128,1]{2,1,0:T(8,128)}, f32[4,128,1]{2,1,0:T(8,128)}, u32[]{:S(2)}, u32[]{:S(2)}) collective-permute-start(f32[4,128,1]{2,1,0:T(8,128)} %get-tuple-element.20), channel_id=1, source_target_pairs={{64,0},{128,64},{192,128},{0,192},{65,1},{129,65},{193,129},{1,193... | collective-permute-start | bytes 6152 | tf_op jit(solution)/shard_map/ppermute | solution.py:18
  37.8 4.4 %collective-permute-start.5 = (f32[10,1,258]{2,1,0:T(1,128)S(1)}, f32[10,1,258]{2,1,0:T(1,128)S(1)}, u32[]{:S(2)}, u32[]{:S(2)}) collective-permute-start(f32[10,1,258]{2,1,0:T(1,128)S(1)} %get-tuple-element.7), channel_id=1, source_target_pairs={{0,1},{1,0},{2,3},{3,2},{4,5},{5,4},{6,7},{7,6},{8,9},{9,8},{10,11... | collective-permute-start | bytes 30968 | tf_op jit(solution)/shard_map/ppermute | solution.py:16
  40.4 3.7 %collective-permute-start.4 = (f32[10,1,258]{2,1,0:T(1,128)S(1)}, f32[10,1,258]{2,1,0:T(1,128)S(1)}, u32[]{:S(2)}, u32[]{:S(2)}) collective-permute-start(f32[10,1,258]{2,1,0:T(1,128)S(1)} %get-tuple-element.6), channel_id=1, source_target_pairs={{1,0},{0,1},{3,2},{2,3},{5,4},{4,5},{7,6},{6,7},{9,8},{8,9},{11,10... | collective-permute-start | bytes 30968 | tf_op jit(solution)/shard_map/ppermute | solution.py:18
  49.1 1.7 %copy-start.1 = (f32[8,256,256]{2,1,0:T(8,128)}, f32[8,256,256]{2,1,0:T(8,128)S(1)}, u32[]{:S(2)}) copy-start(f32[8,256,256]{2,1,0:T(8,128)S(1)} %fusion.2) | copy-start | bytes 6291460
  50.8 5.5 %copy-start.7 = (f32[1,8,256,256]{3,2,1,0:T(8,128)S(1)}, f32[1,8,256,256]{3,2,1,0:T(8,128)}, u32[]{:S(2)}) copy-start(f32[1,8,256,256]{3,2,1,0:T(8,128)} %slice_add_fusion) | copy-start | bytes 6291460
  52.5 6.3 %collective-permute-start.6 = (f32[8,256,1]{1,0,2:T(8,128)S(1)}, f32[8,256,1]{1,0,2:T(8,128)S(1)}, u32[]{:S(2)}, u32[]{:S(2)}) collective-permute-start(f32[8,256,1]{1,0,2:T(8,128)S(1)} %copy.38), channel_id=1, source_target_pairs={{0,64},{64,128},{128,192},{192,0},{1,65},{65,129},{129,193},{193,1... | collective-permute-start | bytes 24584 | tf_op jit(solution)/shard_map/ppermute | solution.py:16
  53.2 6.0 %collective-permute-start.7 = (f32[8,256,1]{1,0,2:T(8,128)S(1)}, f32[8,256,1]{1,0,2:T(8,128)S(1)}, u32[]{:S(2)}, u32[]{:S(2)}) collective-permute-start(f32[8,256,1]{1,0,2:T(8,128)S(1)} %copy.39), channel_id=1, source_target_pairs={{64,0},{128,64},{192,128},{0,192},{65,1},{129,65},{193,129},{1,193... | collective-permute-start | bytes 24584 | tf_op jit(solution)/shard_map/ppermute | solution.py:18
  57.5 3.0 %copy-start.2 = (f32[8,256,256]{2,1,0:T(8,128)S(1)}, f32[8,256,256]{2,1,0:T(8,128)}, u32[]{:S(2)}) copy-start(f32[8,256,256]{2,1,0:T(8,128)} %copy-done.1) | copy-start | bytes 6291460
  60.6 2.0 %copy-start.11 = (f32[4,2,128,256]{3,2,1,0:T(8,128)S(1)}, f32[4,2,128,256]{3,2,1,0:T(8,128)}, u32[]{:S(2)}) copy-start(f32[4,2,128,256]{3,2,1,0:T(8,128)} %reshape.34) | copy-start | bytes 3145732
  62.0 14.3 %copy-start.5 = (f32[8,256,1]{2,1,0:T(8,128)S(1)}, f32[8,256,1]{2,1,0:T(8,128)}, u32[]{:S(2)}) copy-start(f32[8,256,1]{2,1,0:T(8,128)} %copy.41) | copy-start | bytes 24580
  62.0 10.5 %collective-permute-start.8 = (f32[1,256,258]{2,1,0:T(8,128)S(1)}, f32[1,256,258]{2,1,0:T(8,128)S(1)}, u32[]{:S(2)}, u32[]{:S(2)}) collective-permute-start(f32[1,256,258]{2,1,0:T(8,128)S(1)} %get-tuple-element.9), channel_id=1, source_target_pairs={{2,0},{4,2},{6,4},{8,6},{10,8},{12,10},{14,12},{16,14},{18,16},{20... | collective-permute-start | bytes 792584 | tf_op jit(solution)/shard_map/ppermute | solution.py:18
  62.1 14.2 %collective-permute-start.9 = (f32[1,256,258]{2,1,0:T(8,128)S(1)}, f32[1,256,258]{2,1,0:T(8,128)S(1)}, u32[]{:S(2)}, u32[]{:S(2)}) collective-permute-start(f32[1,256,258]{2,1,0:T(8,128)S(1)} %get-tuple-element.8), channel_id=1, source_target_pairs={{0,2},{2,4},{4,6},{6,8},{8,10},{10,12},{12,14},{14,16},{16,18},{18... | collective-permute-start | bytes 792584 | tf_op jit(solution)/shard_map/ppermute | solution.py:16
  64.5 15.6 %collective-permute-start.14 = (f32[1,128,130]{2,1,0:T(8,128)S(1)}, f32[1,128,130]{2,1,0:T(8,128)S(1)}, u32[]{:S(2)}, u32[]{:S(2)}) collective-permute-start(f32[1,128,130]{2,1,0:T(8,128)S(1)} %get-tuple-element.19), channel_id=1, source_target_pairs={{2,0},{4,2},{6,4},{8,6},{10,8},{12,10},{14,12},{16,14},{18,16},{20... | collective-permute-start | bytes 199688 | tf_op jit(solution)/shard_map/ppermute | solution.py:18
  70.2 14.4 %copy-start.4 = (f32[2,8,256,256]{3,2,1,0:T(8,128)S(1)}, f32[2,8,256,256]{3,2,1,0:T(8,128)}, u32[]{:S(2)}) copy-start(f32[2,8,256,256]{3,2,1,0:T(8,128)} %param.3) | copy-start | bytes 12582916
  70.2 10.9 %collective-permute-start.15 = (f32[1,128,130]{2,1,0:T(8,128)S(1)}, f32[1,128,130]{2,1,0:T(8,128)S(1)}, u32[]{:S(2)}, u32[]{:S(2)}) collective-permute-start(f32[1,128,130]{2,1,0:T(8,128)S(1)} %get-tuple-element.18), channel_id=1, source_target_pairs={{0,2},{2,4},{4,6},{6,8},{8,10},{10,12},{12,14},{14,16},{16,18},{18... | collective-permute-start | bytes 199688 | tf_op jit(solution)/shard_map/ppermute | solution.py:16
  76.4 8.2 %collective-permute-start.11 = (f32[10,1,258]{2,1,0:T(1,128)S(1)}, f32[10,1,258]{2,1,0:T(1,128)S(1)}, u32[]{:S(2)}, u32[]{:S(2)}) collective-permute-start(f32[10,1,258]{2,1,0:T(1,128)S(1)} %get-tuple-element.5), channel_id=1, source_target_pairs={{0,1},{1,0},{2,3},{3,2},{4,5},{5,4},{6,7},{7,6},{8,9},{9,8},{10,11... | collective-permute-start | bytes 30968 | tf_op jit(solution)/shard_map/ppermute | solution.py:16
  80.0 4.6 %collective-permute-start.10 = (f32[10,1,258]{2,1,0:T(1,128)S(1)}, f32[10,1,258]{2,1,0:T(1,128)S(1)}, u32[]{:S(2)}, u32[]{:S(2)}) collective-permute-start(f32[10,1,258]{2,1,0:T(1,128)S(1)} %get-tuple-element.4), channel_id=1, source_target_pairs={{1,0},{0,1},{3,2},{2,3},{5,4},{4,5},{7,6},{6,7},{9,8},{8,9},{11,10... | collective-permute-start | bytes 30968 | tf_op jit(solution)/shard_map/ppermute | solution.py:18
  81.0 3.5 %copy-start.13 = (f32[1,128,130]{2,1,0:T(8,128)}, f32[1,128,130]{2,1,0:T(8,128)S(1)}, u32[]{:S(2)}) copy-start(f32[1,128,130]{2,1,0:T(8,128)S(1)} %collective-permute-done.15) | copy-start | bytes 199684
  82.5 10.0 %collective-permute-start.17 = (f32[6,1,130]{2,1,0:T(1,128)}, f32[6,1,130]{2,1,0:T(1,128)}, u32[]{:S(2)}, u32[]{:S(2)}) collective-permute-start(f32[6,1,130]{2,1,0:T(1,128)} %get-tuple-element.17), channel_id=1, source_target_pairs={{0,1},{1,0},{2,3},{3,2},{4,5},{5,4},{6,7},{7,6},{8,9},{9,8},{10,11... | collective-permute-start | bytes 9368 | tf_op jit(solution)/shard_map/ppermute | solution.py:16
  83.5 7.4 %copy-start.15 = (pred[256]{0:T(512)(128)(4,1)S(1)}, pred[256]{0:T(512)(128)(4,1)}, u32[]{:S(2)}) copy-start(pred[256]{0:T(512)(128)(4,1)} %copy-done.14) | copy-start | bytes 772
  83.5 9.0 %collective-permute-start.16 = (f32[6,1,130]{2,1,0:T(1,128)S(1)}, f32[6,1,130]{2,1,0:T(1,128)}, u32[]{:S(2)}, u32[]{:S(2)}) collective-permute-start(f32[6,1,130]{2,1,0:T(1,128)S(1)} %get-tuple-element.16), channel_id=1, source_target_pairs={{1,0},{0,1},{3,2},{2,3},{5,4},{4,5},{7,6},{6,7},{9,8},{8,9},{11,10... | collective-permute-start | bytes 9368 | tf_op jit(solution)/shard_map/ppermute | solution.py:18
  89.6 1.3 %copy-start.8 = (f32[8,256,256]{2,1,0:T(8,128)}, f32[8,256,256]{2,1,0:T(8,128)S(1)}, u32[]{:S(2)}) copy-start(f32[8,256,256]{2,1,0:T(8,128)S(1)} %fusion.5) | copy-start | bytes 6291460
  92.1 1.0 %copy-start.10 = (f32[4,128,256]{2,1,0:T(8,128)S(1)}, f32[4,128,256]{2,1,0:T(8,128)}, u32[]{:S(2)}) copy-start(f32[4,128,256]{2,1,0:T(8,128)} %fusion.24) | copy-start | bytes 1572868
  92.2 1.2 %copy-start.12 = (f32[4,128,256]{2,1,0:T(8,128)S(1)}, f32[4,128,256]{2,1,0:T(8,128)}, u32[]{:S(2)}) copy-start(f32[4,128,256]{2,1,0:T(8,128)} %fusion.23) | copy-start | bytes 1572868
where the time goes:
time: 96.5 us; the launch traced here: 96.1 us
  starting transfers between devices  31.4 us (33%)
  other arithmetic  21.8 us (23%)
  local copies, waits for them, and re-layouts  19.4 us (20%)
  waiting for transfers between devices  18.8 us (19%)
  matrix products  3.78 us (4%)
    ppermute x9, starting transfers between devices, padded_2(): lax.ppermute(head, axis, [((i + 1) % count, i) for i in range(count)])  21.4 us
    ppermute x9, waiting for transfers between devices, padded_2(): lax.ppermute(tail, axis, [(i, (i + 1) % count) for i in range(count)])  10.5 us
    ppermute x9, starting transfers between devices, padded_2(): lax.ppermute(tail, axis, [(i, (i + 1) % count) for i in range(count)])  10 us
    add x2, other arithmetic, advance(): center + spread * (neighbours(padded) - 6.0 * center)  9.99 us
    ppermute x9, waiting for transfers between devices, padded_2(): lax.ppermute(head, axis, [((i + 1) % count, i) for i in range(count)])  8.24 us
    slice x4, local copies, waits for them, and re-layouts, padded_2(): head = lax.slice_in_dim(cells, 0, width, axis=dim)  5.66 us
    unnamed x34, local copies, waits for them, and re-layouts  4.21 us
    concatenate x3, other arithmetic, padded_2(): jnp.concatenate([lax.ppermute(tail, axis, [(i, (i + 1) % count) for i in...  3.85 us
  transfers between devices with their start and end apart: 18, of which 6 were waited for; matrix products, arithmetic and copies ran while one was open for 34% of the time, Pallas kernels for 0%

commit v1 on v0

v1 whole, which is shorter than its diff:
```python
import jax
import jax.numpy as jnp
from jax import lax
from jax.experimental import pallas as pl
from jax.experimental.pallas import tpu as pltpu
from jax.sharding import PartitionSpec as P

F32 = jnp.float32
noise_amp = 0.3
NXB, NYB, NZB = 8, 256, 256
LANES = 128
TOP = 8
PADDED = NYB + 2 * TOP
CHUNK = 64

vmem = pl.BlockSpec(memory_space=pltpu.VMEM)
hbm = pl.BlockSpec(memory_space=pl.ANY)


def lane_iota(rows=CHUNK):
    return lax.broadcasted_iota(jnp.int32, (rows, LANES), 1)


def row_iota(rows=CHUNK):
    return lax.broadcasted_iota(jnp.int32, (rows, LANES), 0)


def pair_table():
    source = lax.broadcasted_iota(jnp.int32, (NZB, LANES), 0) >> 1
    target = lax.broadcasted_iota(jnp.int32, (NZB, LANES), 1)
    return jnp.where(source == target, 1.0, 0.0).astype(jnp.bfloat16)


def pair_lanes(values, table):
    first = values.astype(jnp.bfloat16)
    rest = values - first.astype(F32)
    second = rest.astype(jnp.bfloat16)
    third = (rest - second.astype(F32)).astype(jnp.bfloat16)
    total = jnp.dot(third, table, preferred_element_type=F32)
    total = total + jnp.dot(second, table, preferred_element_type=F32)
    return total + jnp.dot(first, table, preferred_element_type=F32)


def pair_rows(ref, half):
    even = ref[half, pl.ds(0, NYB // 2, stride=2), :]
    odd = ref[half, pl.ds(1, NYB // 2, stride=2), :]
    return even + odd


def pair_both(ref, table):
    return pair_lanes(jnp.concatenate([pair_rows(ref, 0), pair_rows(ref, 1)], axis=1), table)


def beside_lanes(left, right, low, high, lane):
    left_up, left_down = pltpu.roll(left, 1, 1), pltpu.roll(left, LANES - 1, 1)
    right_up, right_down = pltpu.roll(right, 1, 1), pltpu.roll(right, LANES - 1, 1)
    first, last = lane == 0, lane == LANES - 1
    return (
        jnp.where(first, low, left_up) + jnp.where(last, right_down, left_down),
        jnp.where(first, left_up, right_up) + jnp.where(last, high, right_down),
    )


def react(v):
    return v * (0.2 - 0.1 * (v * v))


def parity():
    return lax.rem(lax.axis_index("gz"), 2)


def rows_to_lanes(ref, scratch):
    scratch[0:16, :] = ref[...]
    return [scratch[:, k * LANES : (k + 1) * LANES].T for k in range(2)]


def lanes_to_rows(ref, tiles):
    for k in range(2):
        ref[:, k * LANES : (k + 1) * LANES] = tiles[k].T[0:16]


def start_all(copies):
    for copy in copies:
        copy.start()


def wait_all(copies):
    for copy in copies:
        copy.wait()


def half(k):
    return pl.ds(k * LANES, LANES)


def faces_kernel(u, noise, bp, al, zlo, zhi, yf, planes, forcing, pairs, sems):
    par = parity()
    outer = (par * 7, 7 - par * 7)
    inner = (1 + par * 5, 6 - par * 5)
    spans = ((0, 2), (6, 2), (2, 4))
    field = [
        [
            pltpu.make_async_copy(
                u.at[pl.ds(at, n), :, half(k)], planes.at[pl.ds(at, n), k, pl.ds(TOP, NYB), :], sems.at[2 * i + k]
            )
            for k in range(2)
        ]
        for i, (at, n) in enumerate(spans)
    ]
    force = [
        pltpu.make_async_copy(noise.at[0, 7 * i, :, half(k)], forcing.at[i, k], sems.at[6 + 2 * i + k])
        for i in range(2)
        for k in range(2)
    ]
    start_all(field[0] + field[1] + force + field[2])
    zero = jnp.zeros((8, LANES), F32)
    for x in (0, 7):
        for k in range(2):
            planes[x, k, 0:TOP, :] = zero
            planes[x, k, TOP + NYB :, :] = zero
    table = pair_table()
    lane = lane_iota()
    wait_all(field[0] + field[1] + force)
    for side, (ref, at) in enumerate(((bp, 0), (al, NYB))):
        x, xi = outer[side], inner[side]
        fi = par if side == 0 else 1 - par
        for r in range(0, NYB, CHUNK):
            v = [planes[x, k, TOP + r : TOP + r + CHUNK, :] for k in range(2)]
            z = beside_lanes(v[0], v[1], 0.0, 0.0, lane)
            for k in range(2):
                within = planes[xi, k, TOP + r : TOP + r + CHUNK, :]
                beside = (
                    z[k]
                    + planes[x, k, TOP - 1 + r : TOP - 1 + r + CHUNK, :]
                    + planes[x, k, TOP + 1 + r : TOP + 1 + r + CHUNK, :]
                    + within
                )
                ref[at + r : at + r + CHUNK, half(k)] = (
                    react(v[k]) + 0.15 * beside + noise_amp * forcing[fi, k, r : r + CHUNK, :]
                )
                pairs[k, r : r + CHUNK, :] = v[k] + within
                if side == 1:
                    al[r : r + CHUNK, half(k)] = v[k]
        coarse = pair_both(pairs, table)
        for k in range(2):
            ref[at + NYB : at + NYB + 64, half(k)] = coarse[64 * k : 64 * k + 64]
    wait_all(field[2])
    for x in range(NXB):
        for k in range(2):
            for n, row in enumerate((0, 1, NYB - 1, NYB - 2)):
                yf[8 * n + x : 8 * n + x + 1, half(k)] = planes[x, k, TOP + row : TOP + row + 1, :]
    for k, ref in ((0, zlo), (1, zhi)):
        tiles = []
        for r in range(0, NYB, LANES):
            wide = lane_iota(LANES)
            tile = planes[0, k, TOP + r : TOP + r + LANES, :]
            tile = pltpu.roll(tile, 2, 1) if k else tile
            for x in range(1, NXB):
                moved = pltpu.roll(planes[x, k, TOP + r : TOP + r + LANES, :], 2 * x + 2 * k, 1)
                tile = jnp.where(wide >= 2 * x, moved, tile)
            tiles.append(tile)
        lanes_to_rows(ref, tiles)


def faces(u, noise):
    return pl.pallas_call(
        faces_kernel,
        out_shape=(
            jax.ShapeDtypeStruct((NYB + 64, NZB), F32),
            jax.ShapeDtypeStruct((2 * NYB + 64, NZB), F32),
            jax.ShapeDtypeStruct((16, NYB), F32),
            jax.ShapeDtypeStruct((16, NYB), F32),
            jax.ShapeDtypeStruct((32, NZB), F32),
        ),
        in_specs=[hbm, hbm],
        out_specs=(vmem,) * 5,
        scratch_shapes=[
            pltpu.VMEM((NXB, 2, PADDED, LANES), F32),
            pltpu.VMEM((2, 2, NYB, LANES), F32),
            pltpu.VMEM((2, NYB, LANES), F32),
            pltpu.SemaphoreType.DMA((10,)),
        ],
        name="faces",
    )(u, noise)


def middle_kernel(u, noise, ab, al, glo, ghi, gy, mp, mzlo, mzhi, my, planes, forcing, rows, sems):
    par = parity()
    field = [
        pltpu.make_async_copy(
            u.at[pl.ds(2 * i, 2), :, half(k)], planes.at[pl.ds(2 * i + 1, 2), k, pl.ds(TOP, NYB), :], sems.at[0, 2 * i + k]
        )
        for i in range(4)
        for k in range(2)
    ]
    force = [
        pltpu.make_async_copy(
            noise.at[0, pl.ds(2 * i, 2), :, half(k)], forcing.at[pl.ds(2 * i, 2), k], sems.at[1, 2 * i + k]
        )
        for i in range(4)
        for k in range(2)
    ]
    for i in range(8):
        field[i].start()
        force[i].start()
    for k in range(2):
        planes[par * 9, k, TOP : TOP + NYB, :] = ab[:, half(k)]
        planes[9 - par * 9, k, TOP : TOP + NYB, :] = al[0:NYB, half(k)]
        for x in range(NXB):
            planes[x + 1, k, TOP - 1 : TOP, :] = gy[16 + x : 17 + x, half(k)]
            planes[x + 1, k, TOP + NYB : TOP + NYB + 1, :] = gy[x : x + 1, half(k)]
    low = rows_to_lanes(glo, rows)
    high = rows_to_lanes(ghi, rows)
    lane = lane_iota()
    wait_all(field[0:4] + force[0:2])
    for x in range(NXB):
        if x % 2 == 0 and x > 0:
            wait_all(force[x : x + 2])
            if x < 6:
                wait_all(field[x + 2 : x + 4])
        for r in range(0, NYB, CHUNK):
            at, tile = r % LANES, r // LANES
            v = [planes[x + 1, k, TOP + r : TOP + r + CHUNK, :] for k in range(2)]
            z = beside_lanes(
                v[0],
                v[1],
                pltpu.roll(low[tile][at : at + CHUNK], LANES - (2 * x + 1), 1),
                pltpu.roll(high[tile][at : at + CHUNK], LANES - 1 - 2 * x, 1),
                lane,
            )
            for k in range(2):
                beside = (
                    z[k]
                    + planes[x + 1, k, TOP - 1 + r : TOP - 1 + r + CHUNK, :]
                    + planes[x + 1, k, TOP + 1 + r : TOP + 1 + r + CHUNK, :]
                    + planes[x, k, TOP + r : TOP + r + CHUNK, :]
                    + planes[x + 2, k, TOP + r : TOP + r + CHUNK, :]
                )
                mp[x, k, TOP + r : TOP + r + CHUNK, :] = (
                    react(v[k]) + 0.15 * beside + noise_amp * forcing[x, k, r : r + CHUNK, :]
                )
    for k in range(2):
        for n, row in enumerate((0, NYB - 1)):
            at = TOP + row
            for x in range(NXB):
                my[8 * n + x : 8 * n + x + 1, half(k)] = mp[x, k, at : at + 1, :]
            my[16 + 2 * n : 17 + 2 * n, half(k)] = planes[0, k, at : at + 1, :]
            my[17 + 2 * n : 18 + 2 * n, half(k)] = planes[9, k, at : at + 1, :]
    my[20:24, :] = jnp.zeros((4, NZB), F32)
    wide = lane_iota(LANES)
    for k, ref in ((0, mzlo), (1, mzhi)):
        tiles = []
        for r in range(0, NYB, LANES):
            span = slice(TOP + r, TOP + r + LANES)
            columns = [mp[x, k, span, :] for x in range(NXB)] + [planes[0, k, span, :], planes[9, k, span, :]]
            tile = pltpu.roll(columns[0], 1, 1) if k else columns[0]
            for n in range(1, 10):
                tile = jnp.where(wide >= n, pltpu.roll(columns[n], n + k, 1), tile)
            tiles.append(tile)
        lanes_to_rows(ref, tiles)


def middle(u, noise, ab, al, glo, ghi, gy):
    return pl.pallas_call(
        middle_kernel,
        out_shape=(
            jax.ShapeDtypeStruct((NXB, 2, PADDED, LANES), F32),
            jax.ShapeDtypeStruct((16, NYB), F32),
            jax.ShapeDtypeStruct((16, NYB), F32),
            jax.ShapeDtypeStruct((24, NZB), F32),
        ),
        in_specs=[hbm, hbm] + [vmem] * 5,
        out_specs=(vmem,) * 4,
        scratch_shapes=[
            pltpu.VMEM((NXB + 2, 2, PADDED, LANES), F32),
            pltpu.VMEM((NXB, 2, NYB, LANES), F32),
            pltpu.VMEM((LANES, NYB), F32),
            pltpu.SemaphoreType.DMA((2, 8)),
        ],
        name="middle",
    )(u, noise, ab, al, glo, ghi, gy)


def coarse_kernel(u, noise, glo, ghi, gy, cb, planes, forcing, pairs, sums, ghosts, square, sems):
    field = [
        pltpu.make_async_copy(u.at[pl.ds(2 * i, 2), :, half(k)], planes.at[pl.ds(2 * i, 2), k], sems.at[0, 2 * i + k])
        for i in range(4)
        for k in range(2)
    ]
    force = [
        pltpu.make_async_copy(
            noise.at[0, pl.ds(2 * i, 2), :, half(k)], forcing.at[pl.ds(2 * i, 2), k], sems.at[1, 2 * i + k]
        )
        for i in range(4)
        for k in range(2)
    ]
    start_all(field + force)
    table = pair_table()
    for n, ref in enumerate((glo, ghi)):
        for i in range(4):
            ghosts[8 * n + i : 8 * n + i + 1, :] = (
                ref[4 * i : 4 * i + 1, :] + ref[4 * i + 1 : 4 * i + 2, :] + ref[4 * i + 2 : 4 * i + 3, :] + ref[4 * i + 3 : 4 * i + 4, :]
            )
            at = 16 * (1 - n) + 2 * i
            ghosts[8 * n + 4 + i : 8 * n + 5 + i, :] = (
                gy[at : at + 1, :] + gy[at + 1 : at + 2, :] + gy[at + 8 : at + 9, :] + gy[at + 9 : at + 10, :]
            )
    paired = pair_lanes(ghosts[...], table)
    square[0:16, :] = paired
    for i in range(4):
        sums[i, TOP - 1 : TOP, :] = paired[4 + i : 5 + i]
        sums[i, TOP + LANES : TOP + LANES + 1, :] = paired[12 + i : 13 + i]
    column = square[...].T
    for i in range(4):
        wait_all(field[2 * i : 2 * i + 2])
        for k in range(2):
            pairs[k] = planes[2 * i, k] + planes[2 * i + 1, k]
        sums[i, TOP : TOP + LANES, :] = pair_both(pairs, table)
    lane = lane_iota(LANES)
    for i in range(4):
        wait_all(force[2 * i : 2 * i + 2])
        for k in range(2):
            pairs[k] = forcing[2 * i, k] + forcing[2 * i + 1, k]
        drive = pair_both(pairs, table)
        v = sums[i, TOP : TOP + LANES, :]
        low = pltpu.roll(column, LANES - i, 1) if i else column
        high = pltpu.roll(column, LANES - 1 - (8 + i), 1)
        beside = jnp.where(lane == 0, low, pltpu.roll(v, 1, 1)) + jnp.where(
            lane == LANES - 1, high, pltpu.roll(v, LANES - 1, 1)
        )
        beside = beside + sums[i, TOP - 1 : TOP - 1 + LANES, :] + sums[i, TOP + 1 : TOP + 1 + LANES, :]
        if i > 0:
            beside = beside + sums[i - 1, TOP : TOP + LANES, :]
        if i < 3:
            beside = beside + sums[i + 1, TOP : TOP + LANES, :]
        c = 0.125 * v
        cb[i] = c * (0.2 * (c * c) - 0.75) - (0.075 * 0.125) * beside - (noise_amp * 0.125) * drive


def coarse(u, noise, glo, ghi, gy):
    return pl.pallas_call(
        coarse_kernel,
        out_shape=jax.ShapeDtypeStruct((4, LANES, LANES), F32),
        in_specs=[hbm, hbm] + [vmem] * 3,
        out_specs=vmem,
        scratch_shapes=[
            pltpu.VMEM((NXB, 2, NYB, LANES), F32),
            pltpu.VMEM((NXB, 2, NYB, LANES), F32),
            pltpu.VMEM((2, NYB, LANES), F32),
            pltpu.VMEM((4, LANES + 2 * TOP, LANES), F32),
            pltpu.VMEM((16, NYB), F32),
            pltpu.VMEM((LANES, LANES), F32),
            pltpu.SemaphoreType.DMA((2, 8)),
        ],
        name="coarse",
    )(u, noise, glo, ghi, gy)


def final_kernel(
    u, noise, mp, bp, al, glo, ghi, gy, cb, fine, corr, edges, forcing, ghost, result, pairs, rows, sems, done
):
    par = parity()
    rim = [
        pltpu.make_async_copy(u.at[7 * i, :, half(k)], edges.at[i, k], sems.at[2 * i + k])
        for i in range(2)
        for k in range(2)
    ]
    force = [
        pltpu.make_async_copy(
            noise.at[1, pl.ds(2 * i, 2), :, half(k)], forcing.at[pl.ds(2 * i, 2), k], sems.at[4 + 2 * i + k]
        )
        for i in range(4)
        for k in range(2)
    ]
    start_all(rim + force)
    low = rows_to_lanes(glo, rows)
    high = rows_to_lanes(ghi, rows)
    lane, row = lane_iota(), row_iota()
    table = pair_table()
    first, last = row == 0, row == CHUNK - 1
    wait_all(rim)
    for side, (ref, at) in enumerate(((bp, 0), (al, NYB))):
        i = par if side == 0 else 1 - par
        for r in range(0, NYB, CHUNK):
            tile, span = r // LANES, slice(r % LANES, r % LANES + CHUNK)
            for k in range(2):
                extra = edges[i, k, r : r + CHUNK, :]
                if r == 0:
                    extra = extra + jnp.where(first, jnp.where(i == 0, gy[18:19, half(k)], gy[19:20, half(k)]), 0.0)
                if r == NYB - CHUNK:
                    extra = extra + jnp.where(last, jnp.where(i == 0, gy[16:17, half(k)], gy[17:18, half(k)]), 0.0)
                if k == 0:
                    extra = extra + jnp.where(lane == 0, pltpu.roll(low[tile][span], LANES - 8 - i, 1), 0.0)
                else:
                    extra = extra + jnp.where(lane == LANES - 1, pltpu.roll(high[tile][span], LANES - 1 - 8 - i, 1), 0.0)
                ghost[i, k, r : r + CHUNK, :] = ref[at + r : at + r + CHUNK, half(k)] + 0.15 * extra
    outs = []
    for x in range(NXB):
        if x % 2 == 0:
            wait_all(force[x : x + 2])
        for r in range(0, NYB, CHUNK):
            tile, span = r // LANES, slice(r % LANES, r % LANES + CHUNK)
            v = [mp[x, k, TOP + r : TOP + r + CHUNK, :] for k in range(2)]
            z = beside_lanes(
                v[0],
                v[1],
                pltpu.roll(low[tile][span], LANES - x, 1) if x else low[tile][span],
                pltpu.roll(high[tile][span], LANES - 1 - x, 1),
                lane,
            )
            for k in range(2):
                up = mp[x, k, TOP - 1 + r : TOP - 1 + r + CHUNK, :]
                down = mp[x, k, TOP + 1 + r : TOP + 1 + r + CHUNK, :]
                if r == 0:
                    up = jnp.where(first, gy[8 + x : 9 + x, half(k)], up)
                if r == NYB - CHUNK:
                    down = jnp.where(last, gy[x : x + 1, half(k)], down)
                below = mp[x - 1, k, TOP + r : TOP + r + CHUNK, :] if x > 0 else ghost[0, k, r : r + CHUNK, :]
                above = mp[x + 1, k, TOP + r : TOP + r + CHUNK, :] if x < 7 else ghost[1, k, r : r + CHUNK, :]
                value = react(v[k]) + 0.15 * (z[k] + up + down + below + above)
                result[x, k, r : r + CHUNK, :] = value + noise_amp * forcing[x, k, r : r + CHUNK, :]
                if x % 2 == 0:
                    pairs[k, r : r + CHUNK, :] = value
                else:
                    pairs[k, r : r + CHUNK, :] += value
        for k in range(2):
            out = pltpu.make_async_copy(result.at[x, k], fine.at[x, :, half(k)], done.at[2 * x + k])
            out.start()
            outs.append(out)
        if x % 2 == 1:
            i = x // 2
            total = 0.125 * pair_both(pairs, table) + cb[i]
            if i in (0, 3):
                side_b, side_a = bp[NYB : NYB + 64, :], al[2 * NYB : 2 * NYB + 64, :]
                far = jnp.where(par == (0 if i == 0 else 1), side_b, side_a)
                total = total - (0.075 * 0.125) * jnp.concatenate([far[:, 0:LANES], far[:, LANES:]], axis=0)
            corr[i] = total
    wait_all(outs)


def final(u, noise, mp, bp, al, glo, ghi, gy, cb):
    return pl.pallas_call(
        final_kernel,
        out_shape=(
            jax.ShapeDtypeStruct((NXB, NYB, NZB), F32),
            jax.ShapeDtypeStruct((4, LANES, LANES), F32),
        ),
        in_specs=[hbm, hbm] + [vmem] * 7,
        out_specs=(hbm, vmem),
        scratch_shapes=[
            pltpu.VMEM((2, 2, NYB, LANES), F32),
            pltpu.VMEM((NXB, 2, NYB, LANES), F32),
            pltpu.VMEM((2, 2, NYB, LANES), F32),
            pltpu.VMEM((NXB, 2, NYB, LANES), F32),
            pltpu.VMEM((2, NYB, LANES), F32),
            pltpu.VMEM((LANES, NYB), F32),
            pltpu.SemaphoreType.DMA((12,)),
            pltpu.SemaphoreType.DMA((16,)),
        ],
        name="final",
    )(u, noise, mp, bp, al, glo, ghi, gy, cb)


def swap_pairs(values, axis, first):
    count = lax.axis_size(axis)
    pairs = []
    for i in range(first, count, 2):
        j = (i + 1) % count
        pairs += [(i, j), (j, i)]
    return lax.ppermute(values, axis, pairs)


def shift(values, axis, by):
    count = lax.axis_size(axis)
    return lax.ppermute(values, axis, [(i, (i + by) % count) for i in range(count)])


def on_device(u, noise):
    par = lax.axis_index("gz") % 2
    ab = lax.dynamic_slice_in_dim(u, par * 7, 1, axis=0).reshape(NYB, NZB)
    far_ab = swap_pairs(ab, "gz", 1)
    bp, al, zlo, zhi, yf = faces(u, noise)
    far_bp = swap_pairs(bp, "gz", 1)
    far_al = swap_pairs(al, "gz", 0)
    glo = shift(zhi, "lvl", 1)
    ghi = shift(zlo, "lvl", -1)
    gy = swap_pairs(yf, "gy", 0)
    mp, mzlo, mzhi, my = middle(u, noise, far_ab, far_al, glo, ghi, gy)
    mlo = shift(mzhi, "lvl", 1)
    mhi = shift(mzlo, "lvl", -1)
    mgy = swap_pairs(my, "gy", 0)
    cb = coarse(u, noise, glo, ghi, gy)
    return final(u, noise, mp, far_bp, far_al, mlo, mhi, mgy, cb)


def solution(mesh):
    in_specs = (P("gz", "gy", "lvl"), P(None, "gz", "gy", "lvl"))
    out_specs = (P("gz", "gy", "lvl"), P("gz", "gy", "lvl"))
    return jax.shard_map(on_device, mesh=mesh, in_specs=in_specs, out_specs=out_specs, check_vma=False)
```

time: 96.5 us -> 52.4 us (0.54)
  other arithmetic: 21.8 us -> 0 us
  Pallas kernels: 0 us -> 21.5 us
  local copies, waits for them, and re-layouts: 19.4 us -> 3.17 us
  waiting for transfers between devices: 18.8 us -> 6.86 us
  starting transfers between devices: 31.4 us -> 19.7 us
  matrix products: 3.78 us -> 0 us
    pallas_call x0 -> x4, Pallas kernels: none -> 21.5 us  [the longest x1 7.61 us: final(): pl.pallas_call(final_kernel, out_shape=(jax.ShapeDtypeStruct((NXB, NYB, N...]
    add x6 -> x0, other arithmetic: 13.4 us -> none  [the longest x2 9.99 us: advance(): center + spread * (neighbours(padded) - 6.0 * center)]
    ppermute x18 -> x9, waiting for transfers between devices: 18.8 us -> 6.86 us  [the longest x4 4.72 us: shift(): lax.ppermute(values, axis, [(i, (i + by) % count) for i in range(count)])]
    ppermute x18 -> x9, starting transfers between devices: 31.4 us -> 19.7 us  [the longest x5 13 us: swap_pairs(): return lax.ppermute(values, axis, pairs)]
    slice x5 -> x0, local copies, waits for them, and re-layouts: 7.35 us -> none  [the longest x4 5.66 us: padded_2(): head = lax.slice_in_dim(cells, 0, width, axis=dim)]
    concatenate x3 -> x0, other arithmetic: 3.85 us -> none  [padded_2(): jnp.concatenate([lax.ppermute(tail, axis, [(i, (i + 1) % count) for i in...]
    dot_general x3 -> x0, matrix products: 3.78 us -> none  [coarsen(): jnp.dot(values.reshape(first * second, third), table, precision=lax.Preci...]
    ppermute x4 -> x0, local copies, waits for them, and re-layouts: 3.44 us -> none  [the longest x2 2.71 us: padded_2(): lax.ppermute(head, axis, [((i + 1) % count, i) for i in range(count)])]
  transfers between devices with their start and end apart: 18 -> 9, of which waited for: 6 -> 4; matrix products, arithmetic and copies ran while one was open for 34% -> 2% of each run, Pallas kernels for 0% -> 20%
where the time goes in v1:
time: 52.4 us; the launch traced here: 52.1 us
  Pallas kernels  21.5 us (41%)
  starting transfers between devices  19.7 us (38%)
  waiting for transfers between devices  6.86 us (13%)
  local copies, waits for them, and re-layouts  3.17 us (6%)
  between operations  0.92 us (2%)
    ppermute x5, starting transfers between devices, swap_pairs(): return lax.ppermute(values, axis, pairs)  13 us
    pallas_call x1, Pallas kernels, final(): pl.pallas_call(final_kernel, out_shape=(jax.ShapeDtypeStruct((NXB, NYB, N...  7.61 us
    ppermute x4, starting transfers between devices, shift(): lax.ppermute(values, axis, [(i, (i + by) % count) for i in range(count)])  6.7 us
    pallas_call x1, Pallas kernels, middle(): pl.pallas_call(middle_kernel, out_shape=(jax.ShapeDtypeStruct((NXB, 2, PA...  6.1 us
    ppermute x4, waiting for transfers between devices, shift(): lax.ppermute(values, axis, [(i, (i + by) % count) for i in range(count)])  4.72 us
    pallas_call x1, Pallas kernels, coarse(): pl.pallas_call(coarse_kernel, out_shape=jax.ShapeDtypeStruct((4, LANES, L...  4.52 us
    pallas_call x1, Pallas kernels, faces(): pl.pallas_call(faces_kernel, out_shape=(jax.ShapeDtypeStruct((NYB + 64, N...  3.27 us
    unnamed x18, local copies, waits for them, and re-layouts  2.21 us
  transfers between devices with their start and end apart: 9, of which 4 were waited for; matrix products, arithmetic and copies ran while one was open for 2% of the time, Pallas kernels for 20%

profile of v1, /device:TPU:32, one launch (start us, length us, event | category | flops | bytes accessed | tf_op | source)
XLA Modules:
  0.0 52.1 jit_solution(4436098315662925814)
XLA Ops:
  0.6 3.3 %faces.1 = (f32[320,256]{1,0:T(8,128)}, f32[576,256]{1,0:T(8,128)}, f32[16,256]{1,0:T(8,128)}, f32[16,256]{1,0:T(8,128)}, f32[32,256]{1,0:T(8,128)}) custom-call(f32[8,256,256]{2,1,0:T(8,128)} %u.7, f32[2,8,256,256]{3,2,1,0:T(8,128)} %noise.7), custom_call_target="tpu_custom_call" | custom-call | tf_op jit(solution)/shard_map/faces/pallas_call | solution.py:166
  3.9 0.1 collective-permute-start.1
  4.0 7.7 %collective-permute-start.5 = (f32[320,256]{1,0:T(8,128)}, f32[320,256]{1,0:T(8,128)S(1)}, u32[]{:S(2)}, u32[]{:S(2)}) collective-permute-start(f32[320,256]{1,0:T(8,128)} %get-tuple-element.16), channel_id=1, source_target_pairs={{2,4},{4,2},{6,8},{8,6},{10,12},{12,10},{14,16},{16,14},{18,20},{2... | collective-permute-start | bytes 983048 | tf_op jit(solution)/shard_map/ppermute | solution.py:470
  11.7 1.0 %dynamic-slice_bitcast_fusion = f32[256,256]{1,0:T(8,128)S(1)} fusion(f32[8,256,256]{2,1,0:T(8,128)} %u.7, s32[]{:T(128)S(6)} %select_n.11), kind=kLoop, calls=%fused_computation | loop fusion | bytes 524292 | tf_op jit(solution)/shard_map/reshape | solution.py:480
  12.7 0.1 collective-permute-start
  12.8 1.7 %collective-permute-start.2 = (f32[16,256]{1,0:T(8,128)}, f32[16,256]{1,0:T(8,128)S(1)}, u32[]{:S(2)}, u32[]{:S(2)}) collective-permute-start(f32[16,256]{1,0:T(8,128)} %get-tuple-element.12), channel_id=1, source_target_pairs={{0,64},{64,128},{128,192},{192,0},{1,65},{65,129},{129,193},{193,1... | collective-permute-start | bytes 49160 | tf_op jit(solution)/shard_map/ppermute | solution.py:475
  14.4 1.0 %collective-permute-start.4 = (f32[32,256]{1,0:T(8,128)}, f32[32,256]{1,0:T(8,128)S(1)}, u32[]{:S(2)}, u32[]{:S(2)}) collective-permute-start(f32[32,256]{1,0:T(8,128)} %get-tuple-element.14), channel_id=1, source_target_pairs={{0,1},{1,0},{2,3},{3,2},{4,5},{5,4},{6,7},{7,6},{8,9},{9,8},{10,11... | collective-permute-start | bytes 98312 | tf_op jit(solution)/shard_map/ppermute | solution.py:470
  15.4 2.6 %collective-permute-done.2.glo = f32[16,256]{1,0:T(8,128)S(1)} collective-permute-done((f32[16,256]{1,0:T(8,128)}, f32[16,256]{1,0:T(8,128)S(1)}, u32[]{:S(2)}, u32[]{:S(2)}) %collective-permute-start.2) | collective-permute-done | bytes 16416 | tf_op jit(solution)/shard_map/ppermute | solution.py:475
  18.0 0.0 copy-start.4
  18.0 1.8 %collective-permute-start.3 = (f32[16,256]{1,0:T(8,128)}, f32[16,256]{1,0:T(8,128)S(1)}, u32[]{:S(2)}, u32[]{:S(2)}) collective-permute-start(f32[16,256]{1,0:T(8,128)} %get-tuple-element.13), channel_id=1, source_target_pairs={{0,192},{64,0},{128,64},{192,128},{1,193},{65,1},{129,65},{193,129... | collective-permute-start | bytes 49160 | tf_op jit(solution)/shard_map/ppermute | solution.py:475
  19.8 2.1 %collective-permute-done.3.ghi = f32[16,256]{1,0:T(8,128)S(1)} collective-permute-done((f32[16,256]{1,0:T(8,128)}, f32[16,256]{1,0:T(8,128)S(1)}, u32[]{:S(2)}, u32[]{:S(2)}) %collective-permute-start.3) | collective-permute-done | bytes 16416 | tf_op jit(solution)/shard_map/ppermute | solution.py:475
  22.0 0.0 copy-start.5
  22.0 2.0 %collective-permute-done.4.gy = f32[32,256]{1,0:T(8,128)S(1)} collective-permute-done((f32[32,256]{1,0:T(8,128)}, f32[32,256]{1,0:T(8,128)S(1)}, u32[]{:S(2)}, u32[]{:S(2)}) %collective-permute-start.4) | collective-permute-done | bytes 32800 | tf_op jit(solution)/shard_map/ppermute | solution.py:470
  24.0 0.0 copy-start.3
  24.0 0.1 collective-permute-done.ab
  24.1 0.0 copy-start.2
  24.1 0.0 collective-permute-done.1.al
  24.1 0.0 copy-done.4
  24.1 0.0 copy-done.5
  24.1 0.5 copy-done.3
  24.6 0.2 copy-done.2
  24.8 0.0 copy-start
  24.8 0.8 %copy-done = f32[576,256]{1,0:T(8,128)} copy-done((f32[576,256]{1,0:T(8,128)}, f32[576,256]{1,0:T(8,128)S(1)}, u32[]{:S(2)}) %copy-start) | copy-done | bytes 589848
  25.6 6.1 %middle.1 = (f32[8,2,272,128]{3,2,1,0:T(8,128)}, f32[16,256]{1,0:T(8,128)}, f32[16,256]{1,0:T(8,128)}, f32[24,256]{1,0:T(8,128)}) custom-call(f32[8,256,256]{2,1,0:T(8,128)} %u.7, f32[2,8,256,256]{3,2,1,0:T(8,128)} %noise.7, f32[256,256]{1,0:T(8,128)} %copy-done.2, f32[576,256]{1,0:T(8,128)} %copy-done, f32[16,256]{1,0:T(8,128)} %copy-done.4, ...), custom_call_target="tpu_custom_call" | custom-call | tf_op jit(solution)/shard_map/middle/pallas_call | solution.py:264
  31.8 4.1 %collective-permute-start.8 = (f32[24,256]{1,0:T(8,128)}, f32[24,256]{1,0:T(8,128)S(1)}, u32[]{:S(2)}, u32[]{:S(2)}) collective-permute-start(f32[24,256]{1,0:T(8,128)} %get-tuple-element.19), channel_id=1, source_target_pairs={{0,1},{1,0},{2,3},{3,2},{4,5},{5,4},{6,7},{7,6},{8,9},{9,8},{10,11... | collective-permute-start | bytes 73736 | tf_op jit(solution)/shard_map/ppermute | solution.py:470
  35.8 1.6 %collective-permute-start.6 = (f32[16,256]{1,0:T(8,128)}, f32[16,256]{1,0:T(8,128)S(1)}, u32[]{:S(2)}, u32[]{:S(2)}) collective-permute-start(f32[16,256]{1,0:T(8,128)} %get-tuple-element.17), channel_id=1, source_target_pairs={{0,64},{64,128},{128,192},{192,0},{1,65},{65,129},{129,193},{193,1... | collective-permute-start | bytes 49160 | tf_op jit(solution)/shard_map/ppermute | solution.py:475
  37.4 1.7 %collective-permute-start.7 = (f32[16,256]{1,0:T(8,128)}, f32[16,256]{1,0:T(8,128)S(1)}, u32[]{:S(2)}, u32[]{:S(2)}) collective-permute-start(f32[16,256]{1,0:T(8,128)} %get-tuple-element.18), channel_id=1, source_target_pairs={{0,192},{64,0},{128,64},{192,128},{1,193},{65,1},{129,65},{193,129... | collective-permute-start | bytes 49160 | tf_op jit(solution)/shard_map/ppermute | solution.py:475
  39.1 4.5 %coarse.1.cb = f32[4,128,128]{2,1,0:T(8,128)} custom-call(f32[8,256,256]{2,1,0:T(8,128)} %u.7, f32[2,8,256,256]{3,2,1,0:T(8,128)} %noise.7, f32[16,256]{1,0:T(8,128)} %copy-done.4, f32[16,256]{1,0:T(8,128)} %copy-done.5, f32[32,256]{1,0:T(8,128)} %copy-done.3), custom_call_target="tpu_custom_call" | custom-call | tf_op jit(solution)/shard_map/coarse/pallas_call | solution.py:341
  43.6 0.0 collective-permute-done.5.bp
  43.6 0.0 copy-start.1
  43.6 0.0 collective-permute-done.6.glo
  43.6 0.0 copy-start.7
  43.6 0.0 collective-permute-done.7.ghi
  43.6 0.0 copy-start.8
  43.7 0.0 collective-permute-done.8.gy
  43.7 0.0 copy-start.6
  43.7 0.7 %copy-done.1 = f32[320,256]{1,0:T(8,128)} copy-done((f32[320,256]{1,0:T(8,128)}, f32[320,256]{1,0:T(8,128)S(1)}, u32[]{:S(2)}) %copy-start.1) | copy-done | bytes 327704
  44.3 0.0 copy-done.7
  44.3 0.0 copy-done.8
  44.3 0.0 copy-done.6
  44.4 7.6 %final.1 = (f32[8,256,256]{2,1,0:T(8,128)}, f32[4,128,128]{2,1,0:T(8,128)}) custom-call(f32[8,256,256]{2,1,0:T(8,128)} %u.7, f32[2,8,256,256]{3,2,1,0:T(8,128)} %noise.7, f32[8,2,272,128]{3,2,1,0:T(8,128)} %get-tuple-element.15.mp, f32[320,256]{1,0:T(8,128)} %copy-done.1, f32[576,256]{1,0:T(8,128)} %copy-done, f32[16,256]{1,0:T(8,128)} %copy-done.7, ...), custom_call_target="tpu_custom_call" | custom-call | tf_op jit(solution)/shard_map/final/pallas_call | solution.py:442
Async XLA Ops:
  3.9 20.2 %collective-permute-start.1 = (f32[576,256]{1,0:T(8,128)}, f32[576,256]{1,0:T(8,128)S(1)}, u32[]{:S(2)}, u32[]{:S(2)}) collective-permute-start(f32[576,256]{1,0:T(8,128)} %get-tuple-element.11), channel_id=1, source_target_pairs={{0,2},{2,0},{4,6},{6,4},{8,10},{10,8},{12,14},{14,12},{16,18},{18,... | collective-permute-start | bytes 1769480 | tf_op jit(solution)/shard_map/ppermute | solution.py:470
  4.0 39.6 %collective-permute-start.5 = (f32[320,256]{1,0:T(8,128)}, f32[320,256]{1,0:T(8,128)S(1)}, u32[]{:S(2)}, u32[]{:S(2)}) collective-permute-start(f32[320,256]{1,0:T(8,128)} %get-tuple-element.16), channel_id=1, source_target_pairs={{2,4},{4,2},{6,8},{8,6},{10,12},{12,10},{14,16},{16,14},{18,20},{2... | collective-permute-start | bytes 983048 | tf_op jit(solution)/shard_map/ppermute | solution.py:470
  12.7 11.4 %collective-permute-start = (f32[256,256]{1,0:T(8,128)S(1)}, f32[256,256]{1,0:T(8,128)S(1)}, u32[]{:S(2)}, u32[]{:S(2)}) collective-permute-start(f32[256,256]{1,0:T(8,128)S(1)} %dynamic-slice_bitcast_fusion), channel_id=1, source_target_pairs={{2,4},{4,2},{6,8},{8,6},{10,12},{12,10},{14,16},{16,14},{18,20},{2... | collective-permute-start | bytes 786440 | tf_op jit(solution)/shard_map/ppermute | solution.py:470
  12.8 5.2 %collective-permute-start.2 = (f32[16,256]{1,0:T(8,128)}, f32[16,256]{1,0:T(8,128)S(1)}, u32[]{:S(2)}, u32[]{:S(2)}) collective-permute-start(f32[16,256]{1,0:T(8,128)} %get-tuple-element.12), channel_id=1, source_target_pairs={{0,64},{64,128},{128,192},{192,0},{1,65},{65,129},{129,193},{193,1... | collective-permute-start | bytes 49160 | tf_op jit(solution)/shard_map/ppermute | solution.py:475
  14.4 9.6 %collective-permute-start.4 = (f32[32,256]{1,0:T(8,128)}, f32[32,256]{1,0:T(8,128)S(1)}, u32[]{:S(2)}, u32[]{:S(2)}) collective-permute-start(f32[32,256]{1,0:T(8,128)} %get-tuple-element.14), channel_id=1, source_target_pairs={{0,1},{1,0},{2,3},{3,2},{4,5},{5,4},{6,7},{7,6},{8,9},{9,8},{10,11... | collective-permute-start | bytes 98312 | tf_op jit(solution)/shard_map/ppermute | solution.py:470
  18.0 6.1 %copy-start.4 = (f32[16,256]{1,0:T(8,128)}, f32[16,256]{1,0:T(8,128)S(1)}, u32[]{:S(2)}) copy-start(f32[16,256]{1,0:T(8,128)S(1)} %collective-permute-done.2.glo) | copy-start | bytes 49156
  18.0 3.9 %collective-permute-start.3 = (f32[16,256]{1,0:T(8,128)}, f32[16,256]{1,0:T(8,128)S(1)}, u32[]{:S(2)}, u32[]{:S(2)}) collective-permute-start(f32[16,256]{1,0:T(8,128)} %get-tuple-element.13), channel_id=1, source_target_pairs={{0,192},{64,0},{128,64},{192,128},{1,193},{65,1},{129,65},{193,129... | collective-permute-start | bytes 49160 | tf_op jit(solution)/shard_map/ppermute | solution.py:475
  22.0 2.1 %copy-start.5 = (f32[16,256]{1,0:T(8,128)}, f32[16,256]{1,0:T(8,128)S(1)}, u32[]{:S(2)}) copy-start(f32[16,256]{1,0:T(8,128)S(1)} %collective-permute-done.3.ghi) | copy-start | bytes 49156
  24.0 0.6 %copy-start.3 = (f32[32,256]{1,0:T(8,128)}, f32[32,256]{1,0:T(8,128)S(1)}, u32[]{:S(2)}) copy-start(f32[32,256]{1,0:T(8,128)S(1)} %collective-permute-done.4.gy) | copy-start | bytes 98308
  24.1 0.7 %copy-start.2 = (f32[256,256]{1,0:T(8,128)}, f32[256,256]{1,0:T(8,128)S(1)}, u32[]{:S(2)}) copy-start(f32[256,256]{1,0:T(8,128)S(1)} %collective-permute-done.ab) | copy-start | bytes 786436
  24.8 0.8 %copy-start = (f32[576,256]{1,0:T(8,128)}, f32[576,256]{1,0:T(8,128)S(1)}, u32[]{:S(2)}) copy-start(f32[576,256]{1,0:T(8,128)S(1)} %collective-permute-done.1.al) | copy-start | bytes 1769476
  31.8 11.9 %collective-permute-start.8 = (f32[24,256]{1,0:T(8,128)}, f32[24,256]{1,0:T(8,128)S(1)}, u32[]{:S(2)}, u32[]{:S(2)}) collective-permute-start(f32[24,256]{1,0:T(8,128)} %get-tuple-element.19), channel_id=1, source_target_pairs={{0,1},{1,0},{2,3},{3,2},{4,5},{5,4},{6,7},{7,6},{8,9},{9,8},{10,11... | collective-permute-start | bytes 73736 | tf_op jit(solution)/shard_map/ppermute | solution.py:470
  35.8 7.8 %collective-permute-start.6 = (f32[16,256]{1,0:T(8,128)}, f32[16,256]{1,0:T(8,128)S(1)}, u32[]{:S(2)}, u32[]{:S(2)}) collective-permute-start(f32[16,256]{1,0:T(8,128)} %get-tuple-element.17), channel_id=1, source_target_pairs={{0,64},{64,128},{128,192},{192,0},{1,65},{65,129},{129,193},{193,1... | collective-permute-start | bytes 49160 | tf_op jit(solution)/shard_map/ppermute | solution.py:475
  37.4 6.2 %collective-permute-start.7 = (f32[16,256]{1,0:T(8,128)}, f32[16,256]{1,0:T(8,128)S(1)}, u32[]{:S(2)}, u32[]{:S(2)}) collective-permute-start(f32[16,256]{1,0:T(8,128)} %get-tuple-element.18), channel_id=1, source_target_pairs={{0,192},{64,0},{128,64},{192,128},{1,193},{65,1},{129,65},{193,129... | collective-permute-start | bytes 49160 | tf_op jit(solution)/shard_map/ppermute | solution.py:475
  43.6 0.7 %copy-start.1 = (f32[320,256]{1,0:T(8,128)}, f32[320,256]{1,0:T(8,128)S(1)}, u32[]{:S(2)}) copy-start(f32[320,256]{1,0:T(8,128)S(1)} %collective-permute-done.5.bp) | copy-start | bytes 983044
  43.6 0.7 %copy-start.7 = (f32[16,256]{1,0:T(8,128)}, f32[16,256]{1,0:T(8,128)S(1)}, u32[]{:S(2)}) copy-start(f32[16,256]{1,0:T(8,128)S(1)} %collective-permute-done.6.glo) | copy-start | bytes 49156
  43.6 0.7 %copy-start.8 = (f32[16,256]{1,0:T(8,128)}, f32[16,256]{1,0:T(8,128)S(1)}, u32[]{:S(2)}) copy-start(f32[16,256]{1,0:T(8,128)S(1)} %collective-permute-done.7.ghi) | copy-start | bytes 49156
  43.7 0.7 %copy-start.6 = (f32[24,256]{1,0:T(8,128)}, f32[24,256]{1,0:T(8,128)S(1)}, u32[]{:S(2)}) copy-start(f32[24,256]{1,0:T(8,128)S(1)} %collective-permute-done.8.gy) | copy-start | bytes 73732
